TPU v7x, 32 devices: a whole 2x2x4 slice. The times are simulated.
32 devices in a mesh: rows: 4 (over y, x), feat: 8 (over z, core).
Axes of the slice: x: 2, y: 2, z: 4, core: 2. Of those that a mesh axis runs over, the one named last changes fastest.
Arguments:
- bins: int32 [256, 32768], P(None, ('rows', 'feat')), may hold values from 0 to 255
- leaf: int32 [32768], P(('rows', 'feat')), may hold values from 0 to 1
- grad: bfloat16 [32, 32768], P(None, ('rows', 'feat')), may hold values from -15.55 to 15.55
- hess: bfloat16 [32, 32768], P(None, ('rows', 'feat')), may hold values from 0.049804688 to 1
Outputs:
- gains: float32 [256, 2, 256], P(('rows', 'feat'))
- best: float32 [2], replicated
All inputs are finite; a program needn't handle non-finite values.
Results may differ from a plain program's by a relative error of at most 0.0003.
Values may be sent and summed in bfloat16 or wider, within the bound.
A program may use at most 128 MiB of HBM per device.

v0:
```python
import functools

import jax
import jax.numpy as jnp
from jax import lax
from jax.experimental import pallas as pl
from jax.experimental.pallas import tpu as pltpu
from jax.sharding import PartitionSpec as P

B = 256
LEAVES = 2
LANES = 128
MESH = pl.DeviceIdType.MESH


def add_block(codes, packed, acc_ref, outputs, shard):
    chunks = shard // LANES
    height = 2 * outputs
    both = jnp.concatenate([packed[j * height:(j + 1) * height, :] for j in range(chunks)], axis=1)
    start = chunks * height
    node = jnp.concatenate([packed[start + j:start + j + 1, :] for j in range(chunks)], axis=1)
    zero = jnp.zeros_like(both)
    weighted = jnp.concatenate([jnp.where(node == leaf, both, zero) for leaf in range(LEAVES)], axis=0)
    columns = codes.astype(jnp.float32).T.astype(jnp.bfloat16)
    levels = lax.broadcasted_iota(jnp.int32, (shard, B), 1).astype(jnp.float32).astype(jnp.bfloat16)
    one = jnp.ones((shard, B), jnp.bfloat16)
    none = jnp.zeros((shard, B), jnp.bfloat16)
    for f in range(codes.shape[0]):
        code = jnp.broadcast_to(columns[:, f:f + 1], (shard, B))
        acc_ref[f] += jnp.dot(weighted, jnp.where(code <= levels, one, none), preferred_element_type=jnp.float32)


def feature_gains(cum, outputs):
    rows = []
    for leaf in range(LEAVES):
        base = leaf * 2 * outputs
        left_grad = cum[base:base + outputs]
        left_hess = cum[base + outputs:base + 2 * outputs]
        all_grad = left_grad[:, B - 1:B]
        all_hess = left_hess[:, B - 1:B]
        right_grad = all_grad - left_grad
        right_hess = all_hess - left_hess
        score = (
            left_grad * left_grad / (left_hess + 1.0)
            + right_grad * right_grad / (right_hess + 1.0)
            - all_grad * all_grad / (all_hess + 1.0)
        )
        rows.append(0.5 / outputs * jnp.sum(score, axis=0, keepdims=True))
    return jnp.concatenate(rows, axis=0)


def kernel(sizes, outputs, shard, owned, bins_ref, leaf_ref, grad_ref, hess_ref, gains_ref, best_ref,
           codes_in, codes_all, packed_all, acc_ref, best_all, send_c, recv_c, send_g, recv_g, send_b, recv_b):
    na, nb, nz = sizes
    pairs = na * nb * nz
    count = 2 * pairs
    r = lax.axis_index("rows")
    f = lax.axis_index("feat")
    a, b = r // nb, r % nb
    z, c = f // 2, f % 2

    group = na * nb

    def place(pa, pb, pz, pc):
        return {"rows": pa * nb + pb, "feat": pz * 2 + pc}

    def line(pa, pb, pz, pc):
        return ((pa * nb + pb) * nz + pz) * 2 + pc

    def toggled(dz):
        value, bit = 0, 1
        while bit < nz:
            value = value + (z // bit + dz // bit) % 2 * bit
            bit *= 2
        return value

    def offsets(p, pc):
        da = (1 - pc) * ((p // nb) % na) + pc * (p % na)
        db = (1 - pc) * (p % nb) + pc * ((p // na) % nb)
        return da, db, p // group

    me = line(a, b, z, c)
    other = 1 - c

    def source(p, pc):
        da, db, dz = offsets(p, pc)
        return line((a + da) % na, (b + db) % nb, toggled(dz), pc)

    def target(s):
        da, db, dz = offsets(s // 2, c)
        return (a + na - da) % na, (b + nb - db) % nb, toggled(dz), (c + s) % 2

    rows_size, feat_size = na * nb, nz * 2
    row_at = [lax.rem(r + i, rows_size) for i in range(rows_size)]
    feat_at = [lax.rem(f + i, feat_size) for i in range(feat_size)]
    others = [(i, j) for i in range(rows_size) for j in range(feat_size) if i + j > 0]

    barrier = pltpu.get_barrier_semaphore()
    for i, j in others:
        pl.semaphore_signal(
            barrier, inc=1, device_id={"rows": row_at[i], "feat": feat_at[j]}, device_id_type=MESH)

    chunks = shard // LANES
    own = packed_all.at[me]
    for j in range(chunks):
        part = slice(j * LANES, (j + 1) * LANES)
        own[2 * j * outputs:(2 * j + 1) * outputs] = grad_ref[:, part]
        own[(2 * j + 1) * outputs:(2 * j + 2) * outputs] = hess_ref[:, part]
    node = leaf_ref[...].astype(jnp.float32)
    node = jnp.concatenate([node, jnp.zeros((-chunks % 16, LANES), jnp.float32)], axis=0)
    own[2 * chunks * outputs:] = node.astype(jnp.bfloat16)
    codes_in[...] = bins_ref[...].astype(jnp.float32).astype(jnp.bfloat16).reshape(codes_in.shape)
    codes_all[me] = codes_in[me]
    acc_ref[...] = jnp.zeros_like(acc_ref)

    pl.semaphore_wait(barrier, count - 1)

    def packed_copy(src, slot, sem, where):
        return pltpu.make_async_remote_copy(
            src_ref=src, dst_ref=packed_all.at[slot], send_sem=send_g.at[sem], recv_sem=recv_g.at[slot],
            device_id=where, device_id_type=MESH)

    def codes_copy(s):
        where = target(s)
        return pltpu.make_async_remote_copy(
            src_ref=codes_in.at[line(*where)], dst_ref=codes_all.at[me], send_sem=send_c.at[s],
            recv_sem=recv_c.at[me], device_id=place(*where), device_id_type=MESH)

    def best_copy(i, j):
        return pltpu.make_async_remote_copy(
            src_ref=best_all.at[me], dst_ref=best_all.at[me], send_sem=send_b.at[i * feat_size + j],
            recv_sem=recv_b.at[me], device_id={"rows": row_at[i], "feat": feat_at[j]}, device_id_type=MESH)

    def forward(p, block, slot):
        for core in range(2):
            n1, n2 = (nb, na) if core == 0 else (na, nb)

            def spot(step, k):
                along_b = (step == 1) == (core == 0)
                if along_b:
                    return place(a, (b + nb - k) % nb, z, c)
                return place((a + na - k) % na, b, z, c)

            @pl.when(jnp.logical_and(c == core, (p // n1) % n2 == 0))
            def _():
                for k in range(1, n2):
                    sem = nz * n1 + (p // group * n1 + p % n1) * (n2 - 1) + k - 1
                    packed_copy(block, slot, sem, spot(2, k)).start()

            @pl.when(jnp.logical_and(c == core, p % group == 0))
            def _():
                for k in range(1, n1):
                    packed_copy(block, slot, nz + p // group * (n1 - 1) + k - 1, spot(1, k)).start()

        packed_copy(block, slot, nz * group + p, place(a, b, z, other)).start()

    def take(p):
        slot = source(p, c)
        packed_copy(own, slot, 0, place(a, b, z, other)).wait_recv()
        forward(p, packed_all.at[slot], slot)

    for k in range(1, nz):
        packed_copy(own, me, k, place(a, b, toggled(k), c)).start()
    forward(jnp.int32(0), own, me)

    for s in range(1, count):
        codes_copy(s).start()

    @pl.loop(0, count)
    def _(s):
        p = s // 2
        here = source(p, (c + s) % 2)

        @pl.when(s > 0)
        def _():
            codes_copy_wait = pltpu.make_async_remote_copy(
                src_ref=codes_all.at[here], dst_ref=codes_all.at[here], send_sem=send_c.at[0],
                recv_sem=recv_c.at[here], device_id=place(a, b, z, other), device_id_type=MESH)
            codes_copy_wait.wait_recv()

        @pl.when(s % 2 == 1)
        def _():
            packed_copy(own, here, 0, place(a, b, z, other)).wait_recv()

        add_block(codes_all[here], packed_all[here], acc_ref, outputs, shard)

        @pl.when(jnp.logical_and(s % 2 == 0, jnp.logical_and((p + 1) % group > 0, s + 2 < count)))
        def _():
            take(p + 1)

        @pl.when(jnp.logical_and(s % 2 == 0, jnp.logical_and(p % group == 1, p // group + 1 < nz)))
        def _():
            take((p // group + 1) * group)

    top = None
    for i in range(owned):
        value = feature_gains(acc_ref[i], outputs)
        gains_ref[i] = value
        top = value if top is None else jnp.maximum(top, value)
    peak = jnp.max(top, axis=1, keepdims=True)
    lane = lax.broadcasted_iota(jnp.int32, (1, LANES), 1)
    best_all[me] = jnp.where(lane < LANES // 2, peak[0:1], peak[1:2])

    @pl.loop(1, count)
    def _(s):
        pltpu.make_async_remote_copy(
            src_ref=codes_in.at[0], dst_ref=codes_all.at[0], send_sem=send_c.at[s],
            recv_sem=recv_c.at[0], device_id=place(a, b, z, other), device_id_type=MESH).wait_send()
        packed_copy(own, me, s, place(a, b, z, other)).wait_send()

    for i, j in others:
        best_copy(i, j).start()

    @pl.loop(0, count)
    def _(here):
        @pl.when(here != me)
        def _():
            pltpu.make_async_remote_copy(
                src_ref=best_all.at[here], dst_ref=best_all.at[here], send_sem=send_b.at[0],
                recv_sem=recv_b.at[here], device_id=place(a, b, z, other), device_id_type=MESH).wait_recv()

    for i, j in others:
        best_copy(i, j).wait_send()

    best_ref[...] = jnp.max(best_all[...], axis=0)


def shards(sizes, bins, leaf, grad, hess):
    na, nb, nz = sizes
    count = na * nb * nz * 2
    outputs = grad.shape[0]
    features, shard = bins.shape
    owned = features // count
    chunks = shard // LANES
    packed_rows = chunks * 2 * outputs + chunks + -chunks % 16
    codes_shape = (count, owned, shard)
    dma = pltpu.SemaphoreType.DMA((count,))
    gains, best = pl.pallas_call(
        functools.partial(kernel, sizes, outputs, shard, owned),
        out_shape=(
            jax.ShapeDtypeStruct((owned, LEAVES, B), jnp.float32),
            jax.ShapeDtypeStruct((1, LANES), jnp.float32),
        ),
        in_specs=[pl.BlockSpec(memory_space=pltpu.VMEM)] * 4,
        out_specs=(pl.BlockSpec(memory_space=pltpu.VMEM),) * 2,
        scratch_shapes=[
            pltpu.VMEM(codes_shape, jnp.bfloat16),
            pltpu.VMEM(codes_shape, jnp.bfloat16),
            pltpu.VMEM((count, packed_rows, LANES), jnp.bfloat16),
            pltpu.VMEM((owned, LEAVES * 2 * outputs, B), jnp.float32),
            pltpu.VMEM((count, 1, LANES), jnp.float32),
            dma, dma, dma, dma, dma, dma,
        ],
        compiler_params=pltpu.CompilerParams(
            collective_id=0, has_side_effects=True, vmem_limit_bytes=56 * 1024 * 1024
        ),
    )(bins, leaf.reshape(chunks, LANES), grad, hess)
    return gains, best[0, ::LANES // LEAVES]


def solution(mesh):
    rows, feat = mesh.shape["rows"], mesh.shape["feat"]
    sizes = (rows // 2, 2, feat // 2)
    return jax.shard_map(
        functools.partial(shards, sizes),
        mesh=mesh,
        in_specs=(
            P(None, ("rows", "feat")),
            P(("rows", "feat")),
            P(None, ("rows", "feat")),
            P(None, ("rows", "feat")),
        ),
        out_specs=(P(("rows", "feat"), None, None), P()),
        check_vma=False,
    )
```

profile of v0, /device:TPU:0, one launch (start us, length us, event | category | flops | bytes accessed | tf_op | source)
XLA Modules:
  0.0 60.1 jit_solution(8962267901280215750)
XLA Ops:
  0.6 56.9 %shard_map.59 = (f32[8,2,256]{2,1,0:T(2,128)}, f32[1,128]{1,0:T(1,128)}) custom-call(s32[256,1024]{1,0:T(8,128)} %bins_ref.1, s32[8,128]{1,0:T(8,128)} %bitcast.2, bf16[32,1024]{1,0:T(8,128)(2,1)} %grad_ref.1, bf16[32,1024]{1,0:T(8,128)(2,1)} %hess_ref.1), custom_call_target="tpu_custom_call" | custom-call | tf_op jit(solution)/shard_map/pallas_call | solution.py:238
  57.5 0.0 copy-start
  57.6 0.7 %copy-done = f32[1,128]{1,0:T(1,128)S(1)} copy-done((f32[1,128]{1,0:T(1,128)S(1)}, f32[1,128]{1,0:T(1,128)}, u32[]{:S(2)}) %copy-start) | copy-done | bytes 536
  58.2 0.6 slice.3
  58.8 1.3 %copy.7 = f32[8,2,256]{2,1,0:T(2,128)} copy(f32[8,2,256]{2,1,0:T(2,128)} %get-tuple-element.8) | data formatting | bytes 32768
Async XLA Ops:
  57.5 0.7 %copy-start = (f32[1,128]{1,0:T(1,128)S(1)}, f32[1,128]{1,0:T(1,128)}, u32[]{:S(2)}) copy-start(f32[1,128]{1,0:T(1,128)} %get-tuple-element.5) | copy-start | bytes 1540
where the time goes:
time: 60.4 us; the launch traced here: 60.1 us
  Pallas kernels  56.9 us (94%)
  local copies, waits for them, and re-layouts  2.58 us (4%)
  between operations  0.65 us (1%)
    pallas_call x1, Pallas kernels, shards(): pl.pallas_call(functools.partial(kernel, sizes, outputs, shard, owned), o...  56.9 us
    unnamed x3, local copies, waits for them, and re-layouts  1.98 us

commit v1 on v0

--- a/solution.py
+++ b/solution.py
@@ -10,24 +10,15 @@
 B = 256
 LEAVES = 2
 LANES = 128
+WIDE = 256
+GROUP = 16
+OFFSET = 32768
+AHEAD = 6
 MESH = pl.DeviceIdType.MESH
 
 
-def add_block(codes, packed, acc_ref, outputs, shard):
-    chunks = shard // LANES
-    height = 2 * outputs
-    both = jnp.concatenate([packed[j * height:(j + 1) * height, :] for j in range(chunks)], axis=1)
-    start = chunks * height
-    node = jnp.concatenate([packed[start + j:start + j + 1, :] for j in range(chunks)], axis=1)
-    zero = jnp.zeros_like(both)
-    weighted = jnp.concatenate([jnp.where(node == leaf, both, zero) for leaf in range(LEAVES)], axis=0)
-    columns = codes.astype(jnp.float32).T.astype(jnp.bfloat16)
-    levels = lax.broadcasted_iota(jnp.int32, (shard, B), 1).astype(jnp.float32).astype(jnp.bfloat16)
-    one = jnp.ones((shard, B), jnp.bfloat16)
-    none = jnp.zeros((shard, B), jnp.bfloat16)
-    for f in range(codes.shape[0]):
-        code = jnp.broadcast_to(columns[:, f:f + 1], (shard, B))
-        acc_ref[f] += jnp.dot(weighted, jnp.where(code <= levels, one, none), preferred_element_type=jnp.float32)
+def accumulator(mxu, height):
+    return pltpu.ACC(mxu)((height, B), jnp.float32)
 
 
 def feature_gains(cum, outputs):
@@ -49,8 +40,24 @@
     return jnp.concatenate(rows, axis=0)
 
 
-def kernel(sizes, outputs, shard, owned, bins_ref, leaf_ref, grad_ref, hess_ref, gains_ref, best_ref,
-           codes_in, codes_all, packed_all, acc_ref, best_all, send_c, recv_c, send_g, recv_g, send_b, recv_b):
+def kernel(sizes, outputs, shard, owned, *refs):
+    half = owned // 2
+    height = LEAVES * 2 * outputs
+    pl.run_scoped(
+        functools.partial(body, sizes, outputs, shard, owned, refs),
+        *[accumulator(0, height)] * half,
+        *[accumulator(1, height)] * half,
+        pltpu.VMEM((shard // LANES, height, LANES), jnp.bfloat16),
+        pltpu.VMEM((half, shard, LANES), jnp.int16),
+        pltpu.VMEM((shard, owned), jnp.int16),
+    )
+
+
+def body(sizes, outputs, shard, owned, refs, *scoped):
+    (bins_ref, leaf_ref, grad_ref, hess_ref, gains_ref, best_ref,
+     codes_in, codes_all, packed_all, best_all, send_c, recv_c, send_g, recv_g, send_b, recv_b) = refs
+    accs = scoped[:owned]
+    lhs_ref, tile_ref, cols_ref = scoped[owned:]
     na, nb, nz = sizes
     pairs = na * nb * nz
     count = 2 * pairs
@@ -109,9 +116,63 @@
     node = leaf_ref[...].astype(jnp.float32)
     node = jnp.concatenate([node, jnp.zeros((-chunks % 16, LANES), jnp.float32)], axis=0)
     own[2 * chunks * outputs:] = node.astype(jnp.bfloat16)
-    codes_in[...] = bins_ref[...].astype(jnp.float32).astype(jnp.bfloat16).reshape(codes_in.shape)
-    codes_all[me] = codes_in[me]
-    acc_ref[...] = jnp.zeros_like(acc_ref)
+    codes_in[...] = bins_ref[...].astype(jnp.int16).reshape(codes_in.shape)
+
+    half = owned // 2
+    width = 2 * outputs
+    tiles = [(t, p) for t in range(shard // WIDE) for p in range(half)]
+    lane_id = lax.broadcasted_iota(jnp.int32, (GROUP, LANES), 1)
+    low_top = [(lane_id + h).astype(jnp.int16) for h in range(0, B, LANES)]
+    high_top = [((lane_id + h) * B + (B - 1 - OFFSET)).astype(jnp.int16) for h in range(0, B, LANES)]
+    one = jnp.ones((GROUP, LANES), jnp.bfloat16)
+    none = jnp.zeros((GROUP, LANES), jnp.bfloat16)
+
+    def columns(blocks):
+        parts = []
+        for codes in blocks:
+            wide = codes.astype(jnp.int32)
+            parts.append(wide[:half] + wide[half:] * B - OFFSET)
+        cols_ref[:, :half * len(blocks)] = jnp.concatenate(parts, axis=0).T.astype(jnp.int16)
+
+    def spread(t, p, at):
+        for row in range(t * WIDE, (t + 1) * WIDE, GROUP):
+            tile_ref[p, row:row + GROUP] = jnp.broadcast_to(
+                cols_ref[row:row + GROUP, at + p:at + p + 1], (GROUP, LANES))
+
+    def weigh(where, t):
+        for j in range(t * WIDE // LANES, (t + 1) * WIDE // LANES):
+            both = packed_all[where, j * width:(j + 1) * width]
+            node = packed_all[where, chunks * width + j:chunks * width + j + 1]
+            zero = jnp.zeros_like(both)
+            for leaf in range(LEAVES):
+                lhs_ref[j, leaf * width:(leaf + 1) * width] = jnp.where(node == leaf, both, zero)
+
+    def push(k):
+        t, p = tiles[k % len(tiles)]
+        low, high = [], []
+        for row in range(t * WIDE, (t + 1) * WIDE, GROUP):
+            code = tile_ref[p, row:row + GROUP]
+            rest = code & (B - 1)
+            low.append(jnp.concatenate([jnp.where(rest <= top, one, none) for top in low_top], axis=1))
+            high.append(jnp.concatenate([jnp.where(code <= top, one, none) for top in high_top], axis=1))
+        pltpu.matmul_push_rhs(jnp.concatenate(low, axis=0), k % 2, 0)
+        pltpu.matmul_push_rhs(jnp.concatenate(high, axis=0), k % 2, 1)
+
+    def add_block(later, at):
+        for k, (t, p) in enumerate(tiles):
+            if k + 1 < len(tiles):
+                push(k + 1)
+            span = range(t * WIDE // LANES, (t + 1) * WIDE // LANES)
+            lhs = jnp.concatenate([lhs_ref[j] for j in span], axis=1)
+            pltpu.matmul_acc_lhs(accs[p], lhs, load_staged_rhs=k % 2)
+            pltpu.matmul_acc_lhs(accs[half + p], lhs, load_staged_rhs=k % 2)
+            spread(t, p, at)
+            if p == half - 1:
+                weigh(later, t)
+        push(len(tiles))
+
+    for acc in accs:
+        pltpu.matmul_pop(acc)
 
     pl.semaphore_wait(barrier, count - 1)
 
@@ -163,38 +224,55 @@
         packed_copy(own, me, k, place(a, b, toggled(k), c)).start()
     forward(jnp.int32(0), own, me)
 
-    for s in range(1, count):
+    for s in range(1, min(2 * AHEAD, count)):
         codes_copy(s).start()
 
-    @pl.loop(0, count)
-    def _(s):
-        p = s // 2
-        here = source(p, (c + s) % 2)
-
-        @pl.when(s > 0)
-        def _():
-            codes_copy_wait = pltpu.make_async_remote_copy(
-                src_ref=codes_all.at[here], dst_ref=codes_all.at[here], send_sem=send_c.at[0],
-                recv_sem=recv_c.at[here], device_id=place(a, b, z, other), device_id_type=MESH)
-            codes_copy_wait.wait_recv()
-
-        @pl.when(s % 2 == 1)
-        def _():
-            packed_copy(own, here, 0, place(a, b, z, other)).wait_recv()
-
-        add_block(codes_all[here], packed_all[here], acc_ref, outputs, shard)
-
-        @pl.when(jnp.logical_and(s % 2 == 0, jnp.logical_and((p + 1) % group > 0, s + 2 < count)))
-        def _():
-            take(p + 1)
-
-        @pl.when(jnp.logical_and(s % 2 == 0, jnp.logical_and(p % group == 1, p // group + 1 < nz)))
-        def _():
-            take((p // group + 1) * group)
+    columns([codes_in[me]])
+    for t, p in tiles:
+        spread(t, p, 0)
+        if p == half - 1:
+            weigh(me, t)
+    push(0)
+
+    def wait_codes(here):
+        pltpu.make_async_remote_copy(
+            src_ref=codes_all.at[here], dst_ref=codes_all.at[here], send_sem=send_c.at[0],
+            recv_sem=recv_c.at[here], device_id=place(a, b, z, other), device_id_type=MESH).wait_recv()
+
+    @pl.loop(0, pairs)
+    def _(i):
+        @pl.when(i + AHEAD < pairs)
+        def _():
+            for k in range(2):
+                codes_copy(2 * (i + AHEAD) + k).start()
+
+        @pl.when(jnp.logical_and((i + 1) % group > 0, i + 1 < pairs))
+        def _():
+            take(i + 1)
+
+        @pl.when(jnp.logical_and(i % group == group - 2, i + 2 < pairs))
+        def _():
+            take(i + 2)
+
+        beside = source(i, other)
+        wait_codes(beside)
+        packed_copy(own, beside, 0, place(a, b, z, other)).wait_recv()
+        later = source(jnp.minimum(i + 1, pairs - 1), c)
+
+        @pl.when(i + 1 < pairs)
+        def _():
+            wait_codes(later)
+
+        columns([codes_all[beside], codes_all[later]])
+        add_block(beside, 0)
+        add_block(later, half)
+
+    for acc in (accs[0], accs[half]):
+        pltpu.matmul_acc_lhs(acc, jnp.zeros((LEAVES * width, WIDE), jnp.bfloat16), load_staged_rhs=0)
 
     top = None
     for i in range(owned):
-        value = feature_gains(acc_ref[i], outputs)
+        value = feature_gains(pltpu.matmul_pop(accs[i]), outputs)
         gains_ref[i] = value
         top = value if top is None else jnp.maximum(top, value)
     peak = jnp.max(top, axis=1, keepdims=True)
@@ -244,10 +322,9 @@
         in_specs=[pl.BlockSpec(memory_space=pltpu.VMEM)] * 4,
         out_specs=(pl.BlockSpec(memory_space=pltpu.VMEM),) * 2,
         scratch_shapes=[
-            pltpu.VMEM(codes_shape, jnp.bfloat16),
-            pltpu.VMEM(codes_shape, jnp.bfloat16),
+            pltpu.VMEM(codes_shape, jnp.int16),
+            pltpu.VMEM(codes_shape, jnp.int16),
             pltpu.VMEM((count, packed_rows, LANES), jnp.bfloat16),
-            pltpu.VMEM((owned, LEAVES * 2 * outputs, B), jnp.float32),
             pltpu.VMEM((count, 1, LANES), jnp.float32),
             dma, dma, dma, dma, dma, dma,
         ],

time: 60.4 us -> 57.2 us (0.947)
  Pallas kernels: 56.9 us -> 53.7 us
    pallas_call x1, Pallas kernels: 56.9 us -> 53.7 us  [shards(): pl.pallas_call(functools.partial(kernel, sizes, outputs, shard, owned), o...]
where the time goes in v1:
time: 57.2 us; the launch traced here: 56.9 us
  Pallas kernels  53.7 us (94%)
  local copies, waits for them, and re-layouts  2.58 us (5%)
  between operations  0.65 us (1%)
    pallas_call x1, Pallas kernels, shards(): pl.pallas_call(functools.partial(kernel, sizes, outputs, shard, owned), o...  53.7 us
    unnamed x3, local copies, waits for them, and re-layouts  1.98 us

profile of v1, /device:TPU:0, one launch (start us, length us, event | category | flops | bytes accessed | tf_op | source)
XLA Modules:
  0.0 56.9 jit_solution(18192770870319064216)
XLA Ops:
  0.6 53.7 %shard_map.59 = (f32[8,2,256]{2,1,0:T(2,128)}, f32[1,128]{1,0:T(1,128)}) custom-call(s32[256,1024]{1,0:T(8,128)} %refs_0_.1, s32[8,128]{1,0:T(8,128)} %bitcast.2, bf16[32,1024]{1,0:T(8,128)(2,1)} %refs_2_.1, bf16[32,1024]{1,0:T(8,128)(2,1)} %refs_3_.1), custom_call_target="tpu_custom_call" | custom-call | tf_op jit(solution)/shard_map/pallas_call | solution.py:316
  54.4 0.0 copy-start
  54.4 0.7 %copy-done = f32[1,128]{1,0:T(1,128)S(1)} copy-done((f32[1,128]{1,0:T(1,128)S(1)}, f32[1,128]{1,0:T(1,128)}, u32[]{:S(2)}) %copy-start) | copy-done | bytes 536
  55.0 0.6 %slice.3 = f32[1,2]{1,0:T(1,128)} slice(f32[1,128]{1,0:T(1,128)S(1)} %copy-done), slice={[0:1:1], [0:128:64]} | slice | bytes 16 | tf_op jit(solution)/shard_map/slice | solution.py:335
  55.6 1.3 %copy.7 = f32[8,2,256]{2,1,0:T(2,128)} copy(f32[8,2,256]{2,1,0:T(2,128)} %get-tuple-element.8) | data formatting | bytes 32768
Async XLA Ops:
  54.4 0.7 %copy-start = (f32[1,128]{1,0:T(1,128)S(1)}, f32[1,128]{1,0:T(1,128)}, u32[]{:S(2)}) copy-start(f32[1,128]{1,0:T(1,128)} %get-tuple-element.5) | copy-start | bytes 1540

commit v2 on v1

v2 whole, which is shorter than its diff:
```python
import functools

import jax
import jax.numpy as jnp
from jax import lax
from jax.experimental import pallas as pl
from jax.experimental.pallas import tpu as pltpu
from jax.sharding import PartitionSpec as P

B = 256
LEAVES = 2
LANES = 128
WIDE = 256
GROUP = 16
OFFSET = 32768
AHEAD = 5
PARTS = 2
MESH = pl.DeviceIdType.MESH


def accumulator(mxu, height):
    return pltpu.ACC(mxu)((height, B), jnp.float32)


def feature_gains(cum, outputs):
    rows = []
    for leaf in range(LEAVES):
        base = leaf * 2 * outputs
        left_grad = cum[base:base + outputs]
        left_hess = cum[base + outputs:base + 2 * outputs]
        all_grad = left_grad[:, B - 1:B]
        all_hess = left_hess[:, B - 1:B]
        right_grad = all_grad - left_grad
        right_hess = all_hess - left_hess
        score = (
            left_grad * left_grad / (left_hess + 1.0)
            + right_grad * right_grad / (right_hess + 1.0)
            - all_grad * all_grad / (all_hess + 1.0)
        )
        rows.append(0.5 / outputs * jnp.sum(score, axis=0, keepdims=True))
    return jnp.concatenate(rows, axis=0)


def kernel(sizes, outputs, shard, owned, *refs):
    na, nb, nz = sizes
    half = owned // 2
    height = LEAVES * 2 * outputs
    count = na * nb * nz * 2
    sends = PARTS * (2 * nz + 2 * nz * max(na, nb) * (na + nb))
    dma = pltpu.SemaphoreType.DMA((count,))
    one = pltpu.SemaphoreType.DMA
    pl.run_scoped(
        functools.partial(body, sizes, outputs, shard, owned, refs),
        *[accumulator(0, height)] * half,
        *[accumulator(1, height)] * half,
        pltpu.VMEM((shard // LANES, height, LANES), jnp.bfloat16),
        pltpu.VMEM((half, shard, LANES), jnp.int16),
        pltpu.VMEM((shard, owned), jnp.int16),
        pltpu.SemaphoreType.DMA((2 * shard // LANES + 2,)),
        dma, dma,
        pltpu.SemaphoreType.DMA((sends,)),
        pltpu.SemaphoreType.DMA((count, PARTS)),
        dma, one, one,
    )


def body(sizes, outputs, shard, owned, refs, *scoped):
    (bins_ref, leaf_ref, grad_ref, hess_ref, gains_ref, best_ref,
     bins_in, leaf_in, codes_in, codes_all, packed_all, best_all) = refs
    accs = scoped[:owned]
    (lhs_ref, tile_ref, cols_ref,
     load, send_c, recv_c, send_g, recv_g, send_s, send_b, recv_b) = scoped[owned:]
    na, nb, nz = sizes
    group = na * nb
    pairs = group * nz
    count = 2 * pairs
    chunks = shard // LANES
    half = owned // 2
    width = 2 * outputs
    nodes = chunks + -chunks % 16
    r = lax.axis_index("rows")
    f = lax.axis_index("feat")
    a, b = r // nb, r % nb
    z, c = f // 2, f % 2
    other = 1 - c

    def place(pa, pb, pz, pc):
        return {"rows": pa * nb + pb, "feat": pz * 2 + pc}

    def line(pa, pb, pz, pc):
        return ((pa * nb + pb) * nz + pz) * 2 + pc

    def toggled(dz):
        value, bit = 0, 1
        while bit < nz:
            value = value + lax.rem(lax.div(z, bit) + lax.div(dz, bit), 2) * bit
            bit *= 2
        return value

    def offsets(p, pc):
        p = jnp.int32(p)
        da = (1 - pc) * lax.rem(lax.div(p, nb), na) + pc * lax.rem(p, na)
        db = (1 - pc) * lax.rem(p, nb) + pc * lax.rem(lax.div(p, na), nb)
        return da, db, lax.div(p, group)

    me = line(a, b, z, c)
    beside_me = place(a, b, z, other)

    def source(p, pc):
        da, db, dz = offsets(p, pc)
        return line(lax.rem(a + da, na), lax.rem(b + db, nb), toggled(dz), pc)

    barrier = pltpu.get_barrier_semaphore()

    def greet(where):
        pl.semaphore_signal(barrier, inc=1, device_id=where, device_id_type=MESH)

    for step in (1, -1):
        @pl.when(jnp.logical_and(z + step >= 0, z + step < nz))
        def _():
            for pc in range(2):
                greet(place(a, b, z + step, pc))
    for i in range(na):
        for j in range(nb):
            for k in range(2):
                if i + j + k > 0:
                    greet(place((a + i) % na, (b + j) % nb, z, (c + k) % 2))

    def spots(j):
        start = j * width + (j >= chunks // PARTS) * nodes
        return start, start + outputs, start + width

    node_rows = chunks // PARTS * width
    cuts = [0, node_rows + nodes, chunks * width + nodes]
    loads = [pltpu.make_async_copy(leaf_ref, leaf_in, load.at[2 * chunks])]
    for j in range(chunks):
        part = slice(j * LANES, (j + 1) * LANES)
        start, middle, end = spots(j)
        loads.append(pltpu.make_async_copy(
            grad_ref.at[:, part], packed_all.at[me, start:middle], load.at[2 * j]))
        loads.append(pltpu.make_async_copy(
            hess_ref.at[:, part], packed_all.at[me, middle:end], load.at[2 * j + 1]))
    load_bins = pltpu.make_async_copy(bins_ref, bins_in, load.at[2 * chunks + 1])
    for copy in loads:
        copy.start()
    load_bins.start()

    lane_id = lax.broadcasted_iota(jnp.int32, (GROUP, LANES), 1)
    low_top = [(lane_id + h).astype(jnp.int16) for h in range(0, B, LANES)]
    high_top = [((lane_id + h) * B + (B - 1 - OFFSET)).astype(jnp.int16) for h in range(0, B, LANES)]
    one = jnp.ones((GROUP, LANES), jnp.bfloat16)
    none = jnp.zeros((GROUP, LANES), jnp.bfloat16)
    tiles = [(t, p) for t in range(shard // WIDE) for p in range(half)]

    def columns(blocks):
        parts = []
        for codes in blocks:
            wide = codes.astype(jnp.int32)
            parts.append(wide[:half] + wide[half:] * B - OFFSET)
        cols_ref[:, :half * len(blocks)] = jnp.concatenate(parts, axis=0).T.astype(jnp.int16)

    def spread(t, p, at):
        for row in range(t * WIDE, (t + 1) * WIDE, GROUP):
            tile_ref[p, row:row + GROUP] = jnp.broadcast_to(
                cols_ref[row:row + GROUP, at + p:at + p + 1], (GROUP, LANES))

    def weigh(where, t):
        for j in range(t * WIDE // LANES, (t + 1) * WIDE // LANES):
            start, _, end = spots(j)
            both = packed_all[where, start:end]
            node = packed_all[where, node_rows + j:node_rows + j + 1]
            zero = jnp.zeros_like(both)
            for leaf in range(LEAVES):
                lhs_ref[j, leaf * width:(leaf + 1) * width] = jnp.where(node == leaf, both, zero)

    def push(k):
        t, p = tiles[k % len(tiles)]
        low, high = [], []
        for row in range(t * WIDE, (t + 1) * WIDE, GROUP):
            code = tile_ref[p, row:row + GROUP]
            rest = code & (B - 1)
            low.append(jnp.concatenate([jnp.where(rest <= top, one, none) for top in low_top], axis=1))
            high.append(jnp.concatenate([jnp.where(code <= top, one, none) for top in high_top], axis=1))
        pltpu.matmul_push_rhs(jnp.concatenate(low, axis=0), k % 2, 0)
        pltpu.matmul_push_rhs(jnp.concatenate(high, axis=0), k % 2, 1)

    def add_block(later, at):
        for k, (t, p) in enumerate(tiles):
            if k + 1 < len(tiles):
                push(k + 1)
            span = range(t * WIDE // LANES, (t + 1) * WIDE // LANES)
            lhs = jnp.concatenate([lhs_ref[j] for j in span], axis=1)
            pltpu.matmul_acc_lhs(accs[p], lhs, load_staged_rhs=k % 2)
            pltpu.matmul_acc_lhs(accs[half + p], lhs, load_staged_rhs=k % 2)
            if later is not None:
                spread(t, p, at)
                if p == half - 1:
                    weigh(later, t)
        if later is not None:
            push(len(tiles))

    for acc in accs:
        pltpu.matmul_pop(acc)

    sent = []

    def packed_copy(slot, sem, where, part):
        rows = slice(cuts[part], cuts[part + 1])
        return pltpu.make_async_remote_copy(
            src_ref=packed_all.at[slot, rows], dst_ref=packed_all.at[slot, rows], send_sem=send_g.at[sem],
            recv_sem=recv_g.at[slot, part], device_id=where, device_id_type=MESH)

    def wait_packed(slot, part):
        packed_copy(slot, 0, beside_me, part).wait_recv()

    def send_packed(slot, where, part, when):
        sem = len(sent)
        sent.append((part, when))
        copy = packed_copy(slot, sem, where, part)
        pl.when(when())(copy.start)

    def beside_copy(slot, p):
        return pltpu.make_async_remote_copy(
            src_ref=packed_all.at[slot], dst_ref=packed_all.at[slot], send_sem=send_s.at[p],
            recv_sem=recv_g.at[slot, 0], device_id=beside_me, device_id_type=MESH)

    def send_codes(q, mine=True):
        da, db, dz = offsets(q, c)
        ta, tb, tz = lax.rem(a + na - da, na), lax.rem(b + nb - db, nb), toggled(dz)
        base = line(ta, tb, tz, 0)
        for k in range(0 if mine else 1, 2):
            pc = other if k else c
            pltpu.make_async_remote_copy(
                src_ref=codes_in.at[base + pc], dst_ref=codes_all.at[me], send_sem=send_c.at[2 * q + k],
                recv_sem=recv_c.at[me], device_id=place(ta, tb, tz, pc), device_id_type=MESH).start()

    def is_core(core):
        return c == core

    def passes(step, k):
        origin, there = z - step * k, z + step
        return jnp.logical_and(
            jnp.logical_and(origin >= 0, origin < nz), jnp.logical_and(there >= 0, there < nz))

    def in_plane(g, q, part):
        slot = source(g * group + q, c)
        for core in range(2):
            n1, n2 = (nb, na) if core == 0 else (na, nb)

            def spot(step, k):
                if (step == 1) == (core == 0):
                    return place(a, (b + nb - k) % nb, z, c)
                return place((a + na - k) % na, b, z, c)

            if q < n1:
                for k in range(1, n2):
                    send_packed(slot, spot(2, k), part, functools.partial(is_core, core))
            if q == 0:
                for k in range(1, n1):
                    send_packed(slot, spot(1, k), part, functools.partial(is_core, core))

    def along(k, part):
        for step in (1, -1):
            origin, there = z - step * k, z + step
            inside = jnp.logical_and(origin >= 0, origin < nz)
            slot = line(a, b, origin, c)
            if k > 0:
                @pl.when(inside)
                def _():
                    wait_packed(slot, part)
            send_packed(slot, place(a, b, there, c), part, functools.partial(passes, step, k))

    def relay(g, ahead):
        for part in range(PARTS):
            for q in range(1, early):
                wait_packed(source(g * group + q, c), part)
                in_plane(g, q, part)
            if ahead < nz:
                along(ahead, part)
                in_plane(ahead, 0, part)
        for q in range(1, early):
            beside_copy(source(g * group + q, c), g * group + q).start()
        if ahead < nz:
            beside_copy(source(ahead * group, c), ahead * group).start()

    early = max(na, nb)
    around = 2 * group - 1 + 2 * jnp.where(z > 0, 1, 0) + 2 * jnp.where(z + 1 < nz, 1, 0)

    loads[0].wait()
    node = jnp.concatenate(
        [leaf_in[...].astype(jnp.float32), jnp.zeros((nodes - chunks, LANES), jnp.float32)], axis=0)
    packed_all[me, node_rows:node_rows + nodes] = node.astype(jnp.bfloat16)
    for copy in loads[1:]:
        copy.wait()

    pl.semaphore_wait(barrier, around)

    for part in range(PARTS):
        along(0, part)
        in_plane(0, 0, part)
    beside_copy(me, 0).start()

    load_bins.wait()
    codes_in[...] = bins_in[...].astype(jnp.int16).reshape(codes_in.shape)
    for q in range(min(AHEAD, group)):
        send_codes(q, q > 0)

    def wait_codes(here):
        pltpu.make_async_remote_copy(
            src_ref=codes_all.at[here], dst_ref=codes_all.at[here], send_sem=send_c.at[0],
            recv_sem=recv_c.at[here], device_id=beside_me, device_id_type=MESH).wait_recv()

    def wait_beside(beside):
        wait_codes(beside)
        pltpu.make_async_remote_copy(
            src_ref=packed_all.at[beside], dst_ref=packed_all.at[beside], send_sem=send_s.at[0],
            recv_sem=recv_g.at[beside, 0], device_id=beside_me, device_id_type=MESH).wait_recv()

    columns([codes_in[me]])
    for t, p in tiles:
        spread(t, p, 0)
        if p == half - 1:
            weigh(me, t)
    push(0)

    beside = source(0, other)
    wait_beside(beside)
    columns([codes_all[beside]])
    add_block(beside, 0)
    relay(0, 1)
    for q in range(min(AHEAD, group), min(AHEAD, pairs)):
        send_codes(q)
    later = source(1, c)
    wait_codes(later)
    columns([codes_all[later]])
    add_block(later, 0)

    def step(i, slots):
        beside, later = slots
        for g in range(nz - 1):
            @pl.when(i == g * group + group - 2)
            def _():
                relay(g + 1, g + 2)

        @pl.when(lax.rem(i + 1, group) >= early)
        def _():
            for part in range(PARTS):
                wait_packed(later, part)
            beside_copy(later, i + 1).start()

        @pl.when(i + AHEAD <= pairs)
        def _():
            send_codes(i + AHEAD - 1)

        wait_beside(beside)
        wait_codes(later)
        columns([codes_all[beside], codes_all[later]])
        add_block(beside, 0)
        add_block(later, half)
        return source(i + 1, other), source(i + 2, c)

    beside, _ = lax.fori_loop(1, pairs - 1, step, (source(1, other), source(2, c)))
    wait_beside(beside)
    columns([codes_all[beside]])
    add_block(beside, 0)
    add_block(None, 0)

    top = None
    for i in range(owned):
        value = feature_gains(pltpu.matmul_pop(accs[i]), outputs)
        for h in range(B // LANES):
            row = (i * (B // LANES) + h) * LEAVES
            gains_ref[row:row + LEAVES] = value[:, h * LANES:(h + 1) * LANES]
        top = value if top is None else jnp.maximum(top, value)
    peak = jnp.max(top, axis=1, keepdims=True)
    lane = lax.broadcasted_iota(jnp.int32, (1, LANES), 1)
    best_all[me] = jnp.where(lane == 0, peak[0:1], peak[1:2])

    others = [(i, j) for i in range(group) for j in range(nz * 2) if i + j > 0]
    for i, j in reversed(others):
        pltpu.make_async_remote_copy(
            src_ref=best_all.at[me], dst_ref=best_all.at[me], send_sem=send_b, recv_sem=recv_b,
            device_id={"rows": lax.rem(r + i, group), "feat": lax.rem(f + j, nz * 2)},
            device_id_type=MESH).start()

    @pl.loop(1, count)
    def _(s):
        pltpu.make_async_remote_copy(
            src_ref=codes_in.at[0], dst_ref=codes_all.at[0], send_sem=send_c.at[s],
            recv_sem=recv_c.at[0], device_id=beside_me, device_id_type=MESH).wait_send()

    @pl.loop(0, pairs)
    def _(p):
        beside_copy(me, p).wait_send()

    for sem, (part, when) in enumerate(sent):
        pl.when(when())(packed_copy(me, sem, beside_me, part).wait_send)

    rest = best_all.at[0:count - 1]
    bests = pltpu.make_async_remote_copy(
        src_ref=rest, dst_ref=rest, send_sem=send_b, recv_sem=recv_b,
        device_id=beside_me, device_id_type=MESH)
    bests.wait_recv()
    bests.wait_send()

    best_ref[...] = jnp.max(best_all[...], axis=0)[:, :LEAVES]


def shards(sizes, bins, leaf, grad, hess):
    na, nb, nz = sizes
    count = na * nb * nz * 2
    outputs = grad.shape[0]
    features, shard = bins.shape
    owned = features // count
    chunks = shard // LANES
    packed_rows = chunks * 2 * outputs + chunks + -chunks % 16
    codes_shape = (count, owned, shard)
    halves = B // LANES
    gains, best = pl.pallas_call(
        functools.partial(kernel, sizes, outputs, shard, owned),
        out_shape=(
            jax.ShapeDtypeStruct((owned * halves * LEAVES, LANES), jnp.float32),
            jax.ShapeDtypeStruct((1, LEAVES), jnp.float32),
        ),
        in_specs=[pl.BlockSpec(memory_space=pl.ANY)] * 4,
        out_specs=(pl.BlockSpec(memory_space=pltpu.VMEM),) * 2,
        scratch_shapes=[
            pltpu.VMEM((features, shard), jnp.int32),
            pltpu.VMEM((chunks, LANES), jnp.int32),
            pltpu.VMEM(codes_shape, jnp.int16),
            pltpu.VMEM(codes_shape, jnp.int16),
            pltpu.VMEM((count, packed_rows, LANES), jnp.bfloat16),
            pltpu.VMEM((count, 1, LANES), jnp.float32),
        ],
        compiler_params=pltpu.CompilerParams(
            collective_id=0, has_side_effects=True, vmem_limit_bytes=56 * 1024 * 1024
        ),
    )(bins, leaf.reshape(chunks, LANES), grad, hess)
    gains = gains.reshape(owned, halves, LEAVES, LANES).transpose(0, 2, 1, 3).reshape(owned, LEAVES, B)
    return gains, best.reshape(LEAVES)


def solution(mesh):
    rows, feat = mesh.shape["rows"], mesh.shape["feat"]
    sizes = (rows // 2, 2, feat // 2)
    return jax.shard_map(
        functools.partial(shards, sizes),
        mesh=mesh,
        in_specs=(
            P(None, ("rows", "feat")),
            P(("rows", "feat")),
            P(None, ("rows", "feat")),
            P(None, ("rows", "feat")),
        ),
        out_specs=(P(("rows", "feat"), None, None), P()),
        check_vma=False,
    )
```

time: 57.2 us -> 44 us (0.77)
  Pallas kernels: 53.7 us -> 41.4 us
  local copies, waits for them, and re-layouts: 2.58 us -> 1.84 us
    pallas_call x1, Pallas kernels: 53.7 us -> 41.4 us  [shards(): pl.pallas_call(functools.partial(kernel, sizes, outputs, shard, owned), o...]
    slice x1 -> x0, local copies, waits for them, and re-layouts: 0.6 us -> none  [shards(): return (gains, best[0, ::LANES // LEAVES])]
    unnamed x3 -> x4, local copies, waits for them, and re-layouts: 1.98 us -> 1.84 us
where the time goes in v2:
time: 44 us; the launch traced here: 43.8 us
  Pallas kernels  41.4 us (94%)
  local copies, waits for them, and re-layouts  1.84 us (4%)
  between operations  0.63 us (1%)
    pallas_call x1, Pallas kernels, shards(): pl.pallas_call(functools.partial(kernel, sizes, outputs, shard, owned), o...  41.4 us
    unnamed x4, local copies, waits for them, and re-layouts  1.84 us

profile of v2, /device:TPU:0, one launch (start us, length us, event | category | flops | bytes accessed | tf_op | source)
XLA Modules:
  0.0 43.8 jit_solution(5038644405531422389)
XLA Ops:
  0.6 41.4 %shard_map.59 = (f32[32,128]{1,0:T(8,128)}, f32[1,2]{1,0:T(1,128)}) custom-call(s32[256,1024]{1,0:T(8,128)} %refs_0_.1, s32[8,128]{1,0:T(8,128)} %bitcast.8, bf16[32,1024]{1,0:T(8,128)(2,1)} %refs_2_.1, bf16[32,1024]{1,0:T(8,128)(2,1)} %refs_3_.1), custom_call_target="tpu_custom_call" | custom-call | tf_op jit(solution)/shard_map/pallas_call | solution.py:419
  42.0 0.0 copy-start
  42.0 1.3 %copy.9 = f32[8,2,256]{2,1,0:T(2,128)} copy(f32[8,2,256]{2,1,0:T(2,128)} %bitcast.7) | data formatting | bytes 32768
  43.3 0.0 copy-done
  43.3 0.5 %copy.10 = f32[2]{0:T(128)} copy(f32[2]{0:T(128)S(1)} %bitcast.9) | data formatting | bytes 16
Async XLA Ops:
  42.0 1.3 %copy-start = (f32[1,2]{1,0:T(1,128)S(1)}, f32[1,2]{1,0:T(1,128)}, u32[]{:S(2)}) copy-start(f32[1,2]{1,0:T(1,128)} %get-tuple-element.5) | copy-start | bytes 28

commit v3 on v2

--- a/solution.py
+++ b/solution.py
@@ -13,7 +13,6 @@
 WIDE = 256
 GROUP = 16
 OFFSET = 32768
-AHEAD = 5
 PARTS = 2
 MESH = pl.DeviceIdType.MESH
 
@@ -283,6 +282,13 @@
         if ahead < nz:
             beside_copy(source(ahead * group, c), ahead * group).start()
 
+    def order(n):
+        n = jnp.int32(n)
+        at = lax.rem(n, group)
+        ahead = jnp.logical_and(at == group - 1, n < pairs - 1)
+        behind = jnp.logical_and(at == 0, n > 0)
+        return n + jnp.where(ahead, 1, 0) - jnp.where(behind, 1, 0)
+
     early = max(na, nb)
     around = 2 * group - 1 + 2 * jnp.where(z > 0, 1, 0) + 2 * jnp.where(z + 1 < nz, 1, 0)
 
@@ -302,8 +308,8 @@
 
     load_bins.wait()
     codes_in[...] = bins_in[...].astype(jnp.int16).reshape(codes_in.shape)
-    for q in range(min(AHEAD, group)):
-        send_codes(q, q > 0)
+    for n in range(group + 1):
+        send_codes(order(n), n > 0)
 
     def wait_codes(here):
         pltpu.make_async_remote_copy(
@@ -328,9 +334,7 @@
     columns([codes_all[beside]])
     add_block(beside, 0)
     relay(0, 1)
-    for q in range(min(AHEAD, group), min(AHEAD, pairs)):
-        send_codes(q)
-    later = source(1, c)
+    later = source(order(1), c)
     wait_codes(later)
     columns([codes_all[later]])
     add_block(later, 0)
@@ -338,28 +342,28 @@
     def step(i, slots):
         beside, later = slots
         for g in range(nz - 1):
-            @pl.when(i == g * group + group - 2)
+            @pl.when(i == (g + 1) * (group - 1))
             def _():
                 relay(g + 1, g + 2)
 
-        @pl.when(lax.rem(i + 1, group) >= early)
+        @pl.when(lax.rem(order(i + 1), group) >= early)
         def _():
             for part in range(PARTS):
                 wait_packed(later, part)
-            beside_copy(later, i + 1).start()
-
-        @pl.when(i + AHEAD <= pairs)
+            beside_copy(later, order(i + 1)).start()
+
+        @pl.when(i + (group + 1) <= pairs)
         def _():
-            send_codes(i + AHEAD - 1)
+            send_codes(order(i + (group + 1) - 1))
 
         wait_beside(beside)
         wait_codes(later)
         columns([codes_all[beside], codes_all[later]])
         add_block(beside, 0)
         add_block(later, half)
-        return source(i + 1, other), source(i + 2, c)
-
-    beside, _ = lax.fori_loop(1, pairs - 1, step, (source(1, other), source(2, c)))
+        return source(order(i + 1), other), source(order(i + 2), c)
+
+    beside, _ = lax.fori_loop(1, pairs - 1, step, (source(order(1), other), source(order(2), c)))
     wait_beside(beside)
     columns([codes_all[beside]])
     add_block(beside, 0)
@@ -419,8 +423,8 @@
     gains, best = pl.pallas_call(
         functools.partial(kernel, sizes, outputs, shard, owned),
         out_shape=(
-            jax.ShapeDtypeStruct((owned * halves * LEAVES, LANES), jnp.float32),
-            jax.ShapeDtypeStruct((1, LEAVES), jnp.float32),
+            pltpu.VMEM((owned * halves * LEAVES, LANES), jnp.float32),
+            pltpu.VMEM((1, LEAVES), jnp.float32),
         ),
         in_specs=[pl.BlockSpec(memory_space=pl.ANY)] * 4,
         out_specs=(pl.BlockSpec(memory_space=pltpu.VMEM),) * 2,

time: 44 us -> 41.8 us (0.950)
  Pallas kernels: 41.4 us -> 39.9 us
  local copies, waits for them, and re-layouts: 1.84 us -> 1.12 us
    pallas_call x1, Pallas kernels: 41.4 us -> 39.9 us  [shards(): pl.pallas_call(functools.partial(kernel, sizes, outputs, shard, owned), o...]
    unnamed x4 -> x2, local copies, waits for them, and re-layouts: 1.84 us -> 1.12 us
where the time goes in v3:
time: 41.8 us; the launch traced here: 41.6 us
  Pallas kernels  39.9 us (95%)
  local copies, waits for them, and re-layouts  1.12 us (3%)
  between operations  0.63 us (2%)
    pallas_call x1, Pallas kernels, shards(): pl.pallas_call(functools.partial(kernel, sizes, outputs, shard, owned), o...  39.9 us
    unnamed x2, local copies, waits for them, and re-layouts  1.12 us

profile of v3, /device:TPU:0, one launch (start us, length us, event | category | flops | bytes accessed | tf_op | source)
XLA Modules:
  0.0 41.6 jit_solution(17705013010973124801)
XLA Ops:
  0.6 39.9 %shard_map.59 = (f32[32,128]{1,0:T(8,128)S(1)}, f32[1,2]{1,0:T(1,128)S(1)}) custom-call(s32[256,1024]{1,0:T(8,128)} %refs_0_.1, s32[8,128]{1,0:T(8,128)} %bitcast.9, bf16[32,1024]{1,0:T(8,128)(2,1)} %refs_2_.1, bf16[32,1024]{1,0:T(8,128)(2,1)} %refs_3_.1), custom_call_target="tpu_custom_call" | custom-call | tf_op jit(solution)/shard_map/pallas_call | solution.py:423
  40.5 0.6 %copy.9 = f32[8,2,256]{2,1,0:T(2,128)} copy(f32[8,2,256]{2,1,0:T(2,128)S(1)} %bitcast.7) | data formatting | bytes 32768
  41.1 0.5 %copy.10 = f32[2]{0:T(128)} copy(f32[2]{0:T(128)S(1)} %bitcast.8) | data formatting | bytes 16

commit v4 on v3

--- a/solution.py
+++ b/solution.py
@@ -130,7 +130,7 @@
         return start, start + outputs, start + width
 
     node_rows = chunks // PARTS * width
-    cuts = [0, node_rows + nodes, chunks * width + nodes]
+    cuts = [0] + [k * (chunks // PARTS) * width + nodes for k in range(1, PARTS + 1)]
     loads = [pltpu.make_async_copy(leaf_ref, leaf_in, load.at[2 * chunks])]
     for j in range(chunks):
         part = slice(j * LANES, (j + 1) * LANES)
@@ -172,7 +172,7 @@
             for leaf in range(LEAVES):
                 lhs_ref[j, leaf * width:(leaf + 1) * width] = jnp.where(node == leaf, both, zero)
 
-    def push(k):
+    def push(k, tiles=tiles):
         t, p = tiles[k % len(tiles)]
         low, high = [], []
         for row in range(t * WIDE, (t + 1) * WIDE, GROUP):
@@ -183,20 +183,21 @@
         pltpu.matmul_push_rhs(jnp.concatenate(low, axis=0), k % 2, 0)
         pltpu.matmul_push_rhs(jnp.concatenate(high, axis=0), k % 2, 1)
 
+    def multiply(k, t, p):
+        span = range(t * WIDE // LANES, (t + 1) * WIDE // LANES)
+        lhs = jnp.concatenate([lhs_ref[j] for j in span], axis=1)
+        pltpu.matmul_acc_lhs(accs[p], lhs, load_staged_rhs=k % 2)
+        pltpu.matmul_acc_lhs(accs[half + p], lhs, load_staged_rhs=k % 2)
+
     def add_block(later, at):
         for k, (t, p) in enumerate(tiles):
             if k + 1 < len(tiles):
                 push(k + 1)
-            span = range(t * WIDE // LANES, (t + 1) * WIDE // LANES)
-            lhs = jnp.concatenate([lhs_ref[j] for j in span], axis=1)
-            pltpu.matmul_acc_lhs(accs[p], lhs, load_staged_rhs=k % 2)
-            pltpu.matmul_acc_lhs(accs[half + p], lhs, load_staged_rhs=k % 2)
-            if later is not None:
-                spread(t, p, at)
-                if p == half - 1:
-                    weigh(later, t)
-        if later is not None:
-            push(len(tiles))
+            multiply(k, t, p)
+            spread(t, p, at)
+            if p == half - 1:
+                weigh(later, t)
+        push(len(tiles))
 
     for acc in accs:
         pltpu.matmul_pop(acc)
@@ -271,11 +272,12 @@
 
     def relay(g, ahead):
         for part in range(PARTS):
+            if ahead < nz:
+                along(ahead, part)
             for q in range(1, early):
                 wait_packed(source(g * group + q, c), part)
                 in_plane(g, q, part)
             if ahead < nz:
-                along(ahead, part)
                 in_plane(ahead, 0, part)
         for q in range(1, early):
             beside_copy(source(g * group + q, c), g * group + q).start()
@@ -334,14 +336,20 @@
     columns([codes_all[beside]])
     add_block(beside, 0)
     relay(0, 1)
+    send_codes(order(group + 1))
     later = source(order(1), c)
     wait_codes(later)
     columns([codes_all[later]])
     add_block(later, 0)
 
-    def step(i, slots):
+    first = group + 2
+
+    def step(sending, start, stop, i, slots):
         beside, later = slots
         for g in range(nz - 1):
+            if not start <= (g + 1) * (group - 1) < stop:
+                continue
+
             @pl.when(i == (g + 1) * (group - 1))
             def _():
                 relay(g + 1, g + 2)
@@ -352,30 +360,35 @@
                 wait_packed(later, part)
             beside_copy(later, order(i + 1)).start()
 
-        @pl.when(i + (group + 1) <= pairs)
-        def _():
-            send_codes(order(i + (group + 1) - 1))
-
         wait_beside(beside)
         wait_codes(later)
         columns([codes_all[beside], codes_all[later]])
         add_block(beside, 0)
+        if sending:
+            send_codes(order(i + first - 1))
         add_block(later, half)
         return source(order(i + 1), other), source(order(i + 2), c)
 
-    beside, _ = lax.fori_loop(1, pairs - 1, step, (source(order(1), other), source(order(2), c)))
+    slots = source(order(1), other), source(order(2), c)
+    for sending, start, stop in ((True, 1, pairs - first + 1), (False, pairs - first + 1, pairs - 1)):
+        slots = lax.fori_loop(start, stop, functools.partial(step, sending, start, stop), slots)
+    beside = slots[0]
     wait_beside(beside)
     columns([codes_all[beside]])
     add_block(beside, 0)
-    add_block(None, 0)
-
+    finals = [(t, p) for p in range(half) for t in range(shard // WIDE)]
     top = None
-    for i in range(owned):
-        value = feature_gains(pltpu.matmul_pop(accs[i]), outputs)
-        for h in range(B // LANES):
-            row = (i * (B // LANES) + h) * LEAVES
-            gains_ref[row:row + LEAVES] = value[:, h * LANES:(h + 1) * LANES]
-        top = value if top is None else jnp.maximum(top, value)
+    for k, (t, p) in enumerate(finals):
+        if k + 1 < len(finals):
+            push(k + 1, finals)
+        multiply(k, t, p)
+        if t == shard // WIDE - 1:
+            for i in (p, half + p):
+                value = feature_gains(pltpu.matmul_pop(accs[i]), outputs)
+                for h in range(B // LANES):
+                    row = (i * (B // LANES) + h) * LEAVES
+                    gains_ref[row:row + LEAVES] = value[:, h * LANES:(h + 1) * LANES]
+                top = value if top is None else jnp.maximum(top, value)
     peak = jnp.max(top, axis=1, keepdims=True)
     lane = lax.broadcasted_iota(jnp.int32, (1, LANES), 1)
     best_all[me] = jnp.where(lane == 0, peak[0:1], peak[1:2])

time: 41.8 us -> 41.5 us (level)
  no operation moved by 1% of the time
where the time goes in v4:
time: 41.5 us; the launch traced here: 41.3 us
  Pallas kernels  39.6 us (95%)
  local copies, waits for them, and re-layouts  1.12 us (3%)
  between operations  0.63 us (2%)
    pallas_call x1, Pallas kernels, shards(): pl.pallas_call(functools.partial(kernel, sizes, outputs, shard, owned), o...  39.6 us
    unnamed x2, local copies, waits for them, and re-layouts  1.12 us

profile of v4, /device:TPU:0, one launch (start us, length us, event | category | flops | bytes accessed | tf_op | source)
XLA Modules:
  0.0 41.3 jit_solution(17616977679048423058)
XLA Ops:
  0.6 39.6 %shard_map.59 = (f32[32,128]{1,0:T(8,128)S(1)}, f32[1,2]{1,0:T(1,128)S(1)}) custom-call(s32[256,1024]{1,0:T(8,128)} %refs_0_.1, s32[8,128]{1,0:T(8,128)} %bitcast.9, bf16[32,1024]{1,0:T(8,128)(2,1)} %refs_2_.1, bf16[32,1024]{1,0:T(8,128)(2,1)} %refs_3_.1), custom_call_target="tpu_custom_call" | custom-call | tf_op jit(solution)/shard_map/pallas_call | solution.py:436
  40.2 0.6 %copy.9 = f32[8,2,256]{2,1,0:T(2,128)} copy(f32[8,2,256]{2,1,0:T(2,128)S(1)} %bitcast.7) | data formatting | bytes 32768
  40.8 0.5 %copy.10 = f32[2]{0:T(128)} copy(f32[2]{0:T(128)S(1)} %bitcast.8) | data formatting | bytes 16

commit v5 on v4

--- a/solution.py
+++ b/solution.py
@@ -199,9 +199,6 @@
                 weigh(later, t)
         push(len(tiles))
 
-    for acc in accs:
-        pltpu.matmul_pop(acc)
-
     sent = []
 
     def packed_copy(slot, sem, where, part):
@@ -307,6 +304,9 @@
         along(0, part)
         in_plane(0, 0, part)
     beside_copy(me, 0).start()
+
+    for acc in accs:
+        pltpu.matmul_pop(acc)
 
     load_bins.wait()
     codes_in[...] = bins_in[...].astype(jnp.int16).reshape(codes_in.shape)

time: 41.5 us -> 41.6 us (level)
  no operation moved by 1% of the time
where the time goes in v5:
time: 41.6 us; the launch traced here: 41.4 us
  Pallas kernels  39.6 us (95%)
  local copies, waits for them, and re-layouts  1.12 us (3%)
  between operations  0.63 us (2%)
    pallas_call x1, Pallas kernels, shards(): pl.pallas_call(functools.partial(kernel, sizes, outputs, shard, owned), o...  39.6 us
    unnamed x2, local copies, waits for them, and re-layouts  1.12 us

profile of v5, /device:TPU:0, one launch (start us, length us, event | category | flops | bytes accessed | tf_op | source)
XLA Modules:
  0.0 41.4 jit_solution(744378795169520371)
XLA Ops:
  0.6 39.6 %shard_map.59 = (f32[32,128]{1,0:T(8,128)S(1)}, f32[1,2]{1,0:T(1,128)S(1)}) custom-call(s32[256,1024]{1,0:T(8,128)} %refs_0_.1, s32[8,128]{1,0:T(8,128)} %bitcast.9, bf16[32,1024]{1,0:T(8,128)(2,1)} %refs_2_.1, bf16[32,1024]{1,0:T(8,128)(2,1)} %refs_3_.1), custom_call_target="tpu_custom_call" | custom-call | tf_op jit(solution)/shard_map/pallas_call | solution.py:436
  40.3 0.6 %copy.9 = f32[8,2,256]{2,1,0:T(2,128)} copy(f32[8,2,256]{2,1,0:T(2,128)S(1)} %bitcast.7) | data formatting | bytes 32768
  40.9 0.5 %copy.10 = f32[2]{0:T(128)} copy(f32[2]{0:T(128)S(1)} %bitcast.8) | data formatting | bytes 16
